TPU v7x, 128 devices: a whole 4x4x4 slice. The times are simulated.
128 devices in a mesh: gx: 16 (over z, x), gy: 8 (over y, core).
Axes of the slice: x: 4, y: 4, z: 4, core: 2. Of those that a mesh axis runs over, the one named last changes fastest.
Arguments:
- vectors: float32 [2, 256, 256, 548], P(None, 'gx', 'gy'), may hold values from -6 to 6
- diffusivity: float32 [256, 256], P('gx', 'gy'), may hold values from 0.2 to 0.25
- vertical_factor: float32 [548, 548], replicated, may hold values from -4 to 4, as said below
- weight_first: float32 [548, 768], replicated, may hold values from -0.25 to 0.25
- bias_first: float32 [768], replicated, may hold values from -3 to 3
- weight_second: float32 [768, 768], replicated, may hold values from -0.21875 to 0.21875
- bias_second: float32 [768], replicated, may hold values from -3 to 3
- weight_out: float32 [768, 616], replicated, may hold values from -0.21875 to 0.21875
- error_inverse: float32 [616, 616], replicated, may hold values from -4 to 4, as said below
- observed_column: int32 [65536], P(('gx', 'gy')), may hold values from 0 to 65535, as said below
- owner_count: int32 [128], P(('gx', 'gy')), may hold values from 4 to 512
- observed_state: float32 [65536, 548], P(('gx', 'gy')), may hold values from -6 to 6
- channel_mask: int32 [128, 616], replicated, may hold values 0 or 1
Outputs:
- products: float32 [2, 256, 256, 548], P(None, 'gx', 'gy')
Inputs may be any that keep to these rules, and one draw needn't show every extreme that they name: `observed_column`: tile (a, b) holds the cells i with i // 16 = a and j with j // 32 = b. Among the used slots of one owner at most 4 lie in any one tile, and some tile receives exactly 4 from every owner. Unused slots hold valid columns. `vertical_factor`: the identity plus a dense random part; well conditioned. `error_inverse`: symmetric positive definite with a dominant diagonal.
All inputs are finite; a program needn't handle non-finite values.
Results may differ from a plain program's by a relative error of at most 0.0003.
Values sent between devices are 32-bit elements; how exact they have to be, the bound alone decides.
A program may use at most 128 MiB of HBM per device.

v0:
```python
import functools

import jax
import jax.numpy as jnp
from jax import lax
from jax.experimental import pallas as pl
from jax.experimental.pallas import tpu as pltpu
from jax.sharding import PartitionSpec as P

SWEEPS = 4
LANES = 128
GRID_WIDE = 48
GRID_LEFT = 8
F32 = jnp.float32
BF16 = jnp.bfloat16
MESH = pl.DeviceIdType.MESH
ANY = pl.BlockSpec(memory_space=pl.ANY)
VMEM = pl.BlockSpec(memory_space=pltpu.VMEM)
SMEM = pl.BlockSpec(memory_space=pltpu.SMEM)


def split(x):
    high = x.astype(BF16)
    return high, (x - high.astype(F32)).astype(BF16)


def dot(a, b, transposed=False):
    dims = (((1,), (1 if transposed else 0,)), ((), ()))
    return lax.dot_general(a, b, dims, preferred_element_type=F32)


def dot3(a, b, transposed=False):
    (ah, al), (bh, bl) = a, b
    return dot(ah, bh, transposed) + (dot(ah, bl, transposed) + dot(al, bh, transposed))


def pieces(tile_x, tile_y):
    along, across, corner = SWEEPS * tile_y, SWEEPS * tile_x, SWEEPS * SWEEPS
    first, last, left, right = 0, along, 2 * along, 2 * along + across
    low = across - corner
    sends = (
        ((1, 0), last, along),
        ((-1, 0), first, along),
        ((0, 1), right, across),
        ((0, -1), left, across),
        ((1, 1), right + low, corner),
        ((1, -1), left + low, corner),
        ((-1, 1), right, corner),
        ((-1, -1), left, corner),
    )
    table, start = [], 0
    for step, source, size in sends:
        table.append((step, source, size, start))
        start += size
    return table, start


def pack_kernel(tile, count_ref, column_ref, row_ref, state_ref, vectors_ref, edge_coeff_ref, packed_ref, edges_ref):
    tile_x, tile_y, count_x, count_y = tile
    slots, levels = state_ref.shape
    devices = count_x * count_y
    wide = tile_y * count_y

    def device(column):
        return column // wide // tile_x * count_y + column % wide // tile_y

    columns = row_ref[...]
    target = device(columns)
    cell = columns // wide % tile_x * tile_y + columns % wide % tile_y
    shape = (slots, slots)
    mine = lax.broadcasted_iota(jnp.int32, shape, 1)
    other = lax.broadcasted_iota(jnp.int32, shape, 0)
    used = count_ref[0]
    earlier = (device(column_ref[...]) == target) & (other < used) & (other < mine)
    ordinal = jnp.sum(earlier.astype(F32), axis=0, keepdims=True).astype(jnp.int32)
    live = lax.broadcasted_iota(jnp.int32, (1, slots), 1) < used
    place = (other == jnp.where(live, ordinal * devices + target, slots)).astype(F32)
    label = jnp.sum(place * (cell + 1).astype(F32), axis=1, keepdims=True)
    place = place.astype(BF16)
    high, rest = split(state_ref[...])
    low = (state_ref[...] - high.astype(F32) - rest.astype(F32)).astype(BF16)
    moved = dot(place, high) + (dot(place, rest) + dot(place, low))
    tail = levels % LANES
    parts = -(-(levels + 1) // LANES)
    bucket = slots // devices
    for part in range(parts):
        if part < parts - 1:
            block = moved[:, part * LANES : (part + 1) * LANES]
        else:
            block = jnp.concatenate(
                [
                    moved[:, part * LANES :],
                    label,
                    jnp.zeros((slots, LANES - tail - 1), F32),
                ],
                axis=1,
            )
        for turn in range(bucket):
            packed_ref[pl.ds(turn * parts + part, devices, stride=bucket * parts), :] = block[
                turn * devices : (turn + 1) * devices
            ]

    along, across = SWEEPS * tile_y, SWEEPS * tile_x
    cells = tile_x * tile_y
    for v in range(vectors_ref.shape[0]):
        edges_ref[v, 0:along, 0:levels] = vectors_ref[v, 0:along, :]
        edges_ref[v, along : 2 * along, 0:levels] = vectors_ref[v, cells - along :, :]
        for i in range(tile_x):
            left = vectors_ref[v, i * tile_y : i * tile_y + SWEEPS, :]
            right = vectors_ref[v, (i + 1) * tile_y - SWEEPS : (i + 1) * tile_y, :]
            at = 2 * along + SWEEPS * i
            edges_ref[v, at : at + SWEEPS, 0:levels] = left
            edges_ref[v, at + across : at + across + SWEEPS, 0:levels] = right
        edges_ref[v, :, levels : levels + 1] = edge_coeff_ref[...]


def send_pieces(table, source_at, target_at, sends, receives, back):
    me_x, me_y = lax.axis_index("gx"), lax.axis_index("gy")
    count_x, count_y = lax.axis_size("gx"), lax.axis_size("gy")
    copies = []
    for k, (step, source, size, start) in enumerate(table):
        sign = -1 if back else 1
        peer = {
            "gx": lax.rem(me_x + sign * step[0] + count_x, count_x),
            "gy": lax.rem(me_y + sign * step[1] + count_y, count_y),
        }
        copy = pltpu.make_async_remote_copy(
            src_ref=source_at(source, start, size),
            dst_ref=target_at(source, start, size),
            send_sem=sends.at[k],
            recv_sem=receives.at[k],
            device_id=peer,
            device_id_type=MESH,
        )
        copy.start()
        copies.append(copy)
    return copies


def exchange_kernel(table, edges, packed, halo, carried, sends, receives, all_send, all_recv, own_sem):
    count_y = lax.axis_size("gy")
    devices = lax.axis_size("gx") * count_y
    me = lax.axis_index("gx") * count_y + lax.axis_index("gy")
    rows = lambda ref, start, size: ref.at[:, pl.ds(start, size), :]
    copies = send_pieces(
        table,
        lambda source, start, size: rows(edges, source, size),
        lambda source, start, size: rows(halo, start, size),
        sends,
        receives,
        False,
    )
    own = pltpu.make_async_copy(packed.at[me], carried.at[me], own_sem)
    own.start()

    def send(k, carry):
        peer = lax.rem(me + k, devices)
        pltpu.make_async_remote_copy(
            src_ref=packed.at[peer],
            dst_ref=carried.at[me],
            send_sem=all_send,
            recv_sem=all_recv,
            device_id={"gx": peer // count_y, "gy": lax.rem(peer, count_y)},
            device_id_type=MESH,
        ).start()
        return carry

    lax.fori_loop(1, devices, send, 0)
    own.wait()
    for copy in copies:
        copy.wait()
    others = pl.ds(0, devices - 1)
    every = pltpu.make_async_remote_copy(
        src_ref=packed.at[others],
        dst_ref=carried.at[others],
        send_sem=all_send,
        recv_sem=all_recv,
        device_id={"gx": lax.rem(lax.axis_index("gx") + 1, lax.axis_size("gx"))},
        device_id_type=MESH,
    )
    every.wait()


def return_kernel(table, outward, landed, sends, receives):
    rows = lambda ref, start, size: ref.at[:, pl.ds(start, size), :]
    copies = send_pieces(
        table,
        lambda source, start, size: rows(outward, start, size),
        lambda source, start, size: rows(landed, start, size),
        sends,
        receives,
        True,
    )
    for copy in copies:
        copy.wait()


def spread_rows(tile_x, tile_y):
    at = lambda i, j: (i + SWEEPS) * GRID_WIDE + GRID_LEFT + j
    blocks = [(at(i, 0), tile_y) for i in range(tile_x)]
    blocks += [(at(i - SWEEPS, 0), tile_y) for i in range(SWEEPS)]
    blocks += [(at(i + tile_x, 0), tile_y) for i in range(SWEEPS)]
    blocks += [(at(i, -SWEEPS), SWEEPS) for i in range(tile_x)]
    blocks += [(at(i, tile_y), SWEEPS) for i in range(tile_x)]
    for i0 in (-SWEEPS, tile_x):
        for j0 in (-SWEEPS, tile_y):
            blocks += [(at(i0 + i, j0), SWEEPS) for i in range(SWEEPS)]
    table, start = [], 0
    for source, size in blocks:
        table.append((source, start, size))
        start += size
    return table


def network_kernel(
    tile,
    vectors,
    halo,
    carried,
    coeff,
    mask,
    bias_first,
    bias_second,
    vertical_any,
    first_any,
    second_any,
    out_any,
    inverse_any,
    base,
    outward,
    vertical,
    first,
    second,
    out,
    inverse,
    grid_coeff,
    grid,
    spread,
    lifted,
    spread_high,
    spread_low,
    smooth_high,
    smooth_low,
    slope_one,
    slope_two,
    gate,
    sems,
):
    tile_x, tile_y, count_x, count_y = tile
    cells = tile_x * tile_y
    levels = vectors.shape[2]
    loads = []
    for k, (source, target) in enumerate(
        (
            (vertical_any, vertical),
            (first_any, first),
            (second_any, second),
            (out_any, out),
            (inverse_any, inverse),
        )
    ):
        load = pltpu.make_async_copy(source, target, sems.at[k])
        load.start()
        loads.append(load)

    order = spread_rows(tile_x, tile_y)
    grid_coeff[...] = jnp.zeros(grid_coeff.shape, F32)
    for source, start, size in order:
        if start < cells:
            column = coeff[start : start + size, :]
        else:
            column = halo[0, start - cells : start - cells + size, levels : levels + 1]
        grid_coeff[source : source + size, :] = jnp.broadcast_to(column, (size, LANES))
    chunk_x = LANES // tile_y
    near = (chunk_x + 2 * SWEEPS) * GRID_WIDE
    me_x, me_y = lax.axis_index("gx") * tile_x, lax.axis_index("gy") * tile_y
    grid[...] = jnp.zeros(grid.shape, F32)
    for q in range(tile_x // chunk_x):
        row = lax.broadcasted_iota(jnp.int32, (near, LANES), 0)
        lane = lax.broadcasted_iota(jnp.int32, (near, LANES), 1)
        i, j = row // GRID_WIDE - SWEEPS, row % GRID_WIDE - GRID_LEFT
        x, y = i + q * chunk_x + me_x, j + me_y
        inside = (x >= 0) & (x < tile_x * count_x) & (y >= 0) & (y < tile_y * count_y)
        begin = q * chunk_x * GRID_WIDE
        scale = jnp.where(inside, grid_coeff[begin : begin + near, :], 0.0)
        field = ((i == lane // tile_y) & (j == lane % tile_y)).astype(F32)
        for _ in range(SWEEPS):
            scaled = scale * field
            beside = (
                pltpu.roll(scaled, 1, 0)
                + pltpu.roll(scaled, near - 1, 0)
                + pltpu.roll(scaled, GRID_WIDE, 0)
                + pltpu.roll(scaled, near - GRID_WIDE, 0)
            )
            field = field + beside - 4.0 * scaled
        grid[begin : begin + near, q * LANES : (q + 1) * LANES] = jnp.where(inside, field, 0.0)
    for source, start, size in order:
        spread[start : start + size, :] = grid[source : source + size, :]
    total = order[-1][1] + order[-1][2]
    spread[total:, :] = jnp.zeros((spread.shape[0] - total, cells), F32)
    spread_high[...], spread_low[...] = split(spread[0:total, :])
    smooth_high[...], smooth_low[...] = split(jnp.transpose(spread[...]))

    loads[0].wait()
    loads[1].wait()
    first_split = split(first[...])
    lifted[...] = dot3(split(jnp.transpose(vertical[...])), first_split)

    devices = mask.shape[0]
    parts = -(-(levels + 1) // LANES)
    turns = carried.shape[0] // (devices * parts)
    tail = levels % LANES
    profile, label = [], []
    for turn in range(turns):
        blocks = [
            carried[pl.ds(turn * parts + part, devices, stride=turns * parts), :]
            for part in range(parts)
        ]
        label.append(blocks[-1][:, tail : tail + 1])
        profile.append(jnp.concatenate(blocks, axis=1)[:, 0:levels])
    profile = jnp.concatenate(profile, axis=0)
    slots = turns * devices
    gate_mask = mask[...].astype(F32)
    picks = []
    for turn in range(turns):
        live = (label[turn] > 0.5).astype(F32)
        gate[turn * devices : (turn + 1) * devices, :] = gate_mask * live
        across = jnp.transpose(jnp.broadcast_to(label[turn], (devices, LANES)))[0:1, :]
        picks.append(across)
    asked_row = jnp.concatenate(picks, axis=1)
    asked_column = jnp.concatenate(label, axis=0)
    number = lax.broadcasted_iota(jnp.int32, (slots, cells), 1).astype(F32) + 1.0
    pick = (jnp.abs(number - asked_column) < 0.5).astype(F32).astype(BF16)
    number = lax.broadcasted_iota(jnp.int32, (cells, slots), 0).astype(F32) + 1.0
    put = (jnp.abs(number - asked_row) < 0.5).astype(F32).astype(BF16)

    hidden = jnp.tanh(dot3(split(profile), first_split) + bias_first[...])
    slope_one[...] = 1.0 - hidden * hidden
    loads[2].wait()
    second_split = split(second[...])
    hidden = jnp.tanh(dot3(split(hidden), second_split) + bias_second[...])
    slope_two[...] = 1.0 - hidden * hidden
    loads[3].wait()
    loads[4].wait()

    def one_vector(v, carry):
        own = (smooth_high[:, 0:cells], smooth_low[:, 0:cells])
        around = (smooth_high[:, cells:total], smooth_low[:, cells:total])
        smooth = dot3(own, split(vectors[v])) + dot3(around, split(halo[v, :, 0:levels]))
        lifted_split = split(lifted[...])
        at_cells = dot3(split(smooth), lifted_split)
        high, low = split(at_cells)
        tangent = (dot(pick, high) + dot(pick, low)) * slope_one[...]
        weight = split(second[...])
        tangent = dot3(split(tangent), weight) * slope_two[...]
        weight = split(out[...])
        tangent = dot3(split(tangent), weight) * gate[...]
        weighted = dot3(split(tangent), split(inverse[...])) * gate[...]
        gradient = dot3(split(weighted), weight, True) * slope_two[...]
        weight = split(second[...])
        gradient = dot3(split(gradient), weight, True) * slope_one[...]
        high, low = split(gradient)
        gradient = dot(put, high) + dot(put, low)
        gradient = split(dot3(split(gradient), lifted_split, True))
        base[v] = vectors[v] + dot3((spread_high[0:cells, :], spread_low[0:cells, :]), gradient)
        outward[v] = dot3((spread_high[cells:total, :], spread_low[cells:total, :]), gradient)
        return carry

    lax.fori_loop(0, vectors.shape[0], one_vector, 0)


def finish_kernel(tile, base, landed, result):
    tile_x, tile_y, _, _ = tile
    cells = tile_x * tile_y
    along, across = SWEEPS * tile_y, SWEEPS * tile_x
    for v in range(base.shape[0]):
        result[v] = base[v]
        result[v, cells - along :, :] += landed[v, 0:along, :]
        result[v, 0:along, :] += landed[v, along : 2 * along, :]
        corners = 2 * along + 2 * across
        size = SWEEPS * SWEEPS
        for i in range(tile_x):
            start = 2 * along + SWEEPS * i
            right = landed[v, start : start + SWEEPS, :]
            left = landed[v, start + across : start + across + SWEEPS, :]
            if i < SWEEPS:
                at = corners + SWEEPS * i
                left += landed[v, at + 3 * size : at + 3 * size + SWEEPS, :]
                right += landed[v, at + 2 * size : at + 2 * size + SWEEPS, :]
            if i >= tile_x - SWEEPS:
                at = corners + SWEEPS * (i - tile_x + SWEEPS)
                left += landed[v, at + size : at + size + SWEEPS, :]
                right += landed[v, at : at + SWEEPS, :]
            result[v, i * tile_y : i * tile_y + SWEEPS, :] += left
            result[v, (i + 1) * tile_y - SWEEPS : (i + 1) * tile_y, :] += right


def shaped(*shape):
    return jax.ShapeDtypeStruct(shape, F32)


LIMIT = 60 * 1024 * 1024


def body(
    vectors,
    diffusivity,
    vertical_factor,
    weight_first,
    bias_first,
    weight_second,
    bias_second,
    weight_out,
    error_inverse,
    observed_column,
    owner_count,
    observed_state,
    channel_mask,
):
    pairs, tile_x, tile_y, levels = vectors.shape
    units, channels = weight_out.shape
    count_x = lax.axis_size("gx")
    count_y = lax.axis_size("gy")
    devices = count_x * count_y
    tile = (tile_x, tile_y, count_x, count_y)
    slots = observed_column.shape[0]
    bucket = slots // devices
    cells = tile_x * tile_y
    parts = -(-(levels + 1) // LANES)
    table, halo_rows = pieces(tile_x, tile_y)
    flat = vectors.reshape(pairs, cells, levels)
    coeff = diffusivity.reshape(cells, 1)
    edge_coeff = jnp.concatenate(
        [
            diffusivity[:SWEEPS].reshape(-1),
            diffusivity[-SWEEPS:].reshape(-1),
            diffusivity[:, :SWEEPS].reshape(-1),
            diffusivity[:, -SWEEPS:].reshape(-1),
        ]
    )[:, None]
    edge_rows = edge_coeff.shape[0]

    packed, edges = pl.pallas_call(
        functools.partial(pack_kernel, tile),
        out_shape=(shaped(slots * parts, LANES), shaped(pairs, edge_rows, levels + 1)),
        in_specs=[SMEM] + [VMEM] * 5,
        out_specs=(VMEM, VMEM),
        compiler_params=pltpu.CompilerParams(vmem_limit_bytes=LIMIT),
    )(owner_count, observed_column[:, None], observed_column[None, :], observed_state, flat, edge_coeff)

    dma = pltpu.SemaphoreType.DMA
    halo, carried = pl.pallas_call(
        functools.partial(exchange_kernel, table),
        out_shape=(
            shaped(pairs, halo_rows, levels + 1),
            shaped(devices, 1, bucket * parts * LANES),
        ),
        in_specs=[ANY, ANY],
        out_specs=(ANY, ANY),
        scratch_shapes=[dma((8,)), dma((8,)), dma, dma, dma],
        compiler_params=pltpu.CompilerParams(has_side_effects=True),
    )(edges, packed.reshape(devices, 1, bucket * parts * LANES))

    vm = pltpu.VMEM
    grid_rows = (tile_x + 2 * SWEEPS) * GRID_WIDE
    total = cells + halo_rows
    padded = -(-total // LANES) * LANES
    base, outward = pl.pallas_call(
        functools.partial(network_kernel, tile),
        out_shape=(shaped(pairs, cells, levels), shaped(pairs, halo_rows, levels)),
        in_specs=[VMEM] * 7 + [ANY] * 5,
        out_specs=(VMEM, VMEM),
        scratch_shapes=[
            vm((levels, levels), F32),
            vm((levels, units), F32),
            vm((units, units), F32),
            vm((units, channels), F32),
            vm((channels, channels), F32),
            vm((grid_rows, LANES), F32),
            vm((grid_rows, cells), F32),
            vm((padded, cells), F32),
            vm((levels, units), F32),
            vm((total, cells), BF16),
            vm((total, cells), BF16),
            vm((cells, padded), BF16),
            vm((cells, padded), BF16),
            vm((slots, units), F32),
            vm((slots, units), F32),
            vm((slots, channels), F32),
            dma((5,)),
        ],
        compiler_params=pltpu.CompilerParams(vmem_limit_bytes=LIMIT),
    )(
        flat,
        halo,
        carried.reshape(slots * parts, LANES),
        coeff,
        channel_mask,
        bias_first[None, :],
        bias_second[None, :],
        vertical_factor,
        weight_first,
        weight_second,
        weight_out,
        error_inverse,
    )

    landed = pl.pallas_call(
        functools.partial(return_kernel, table),
        out_shape=shaped(pairs, halo_rows, levels),
        in_specs=[ANY],
        out_specs=ANY,
        scratch_shapes=[dma((8,)), dma((8,))],
        compiler_params=pltpu.CompilerParams(has_side_effects=True),
    )(outward)

    result = pl.pallas_call(
        functools.partial(finish_kernel, tile),
        out_shape=shaped(pairs, cells, levels),
        in_specs=[VMEM, VMEM],
        out_specs=VMEM,
        compiler_params=pltpu.CompilerParams(vmem_limit_bytes=LIMIT),
    )(base, landed)
    return result.reshape(vectors.shape)


def solution(mesh):
    in_specs = (
        P(None, "gx", "gy", None),
        P("gx", "gy"),
        P(),
        P(),
        P(),
        P(),
        P(),
        P(),
        P(),
        P(("gx", "gy")),
        P(("gx", "gy")),
        P(("gx", "gy"), None),
        P(),
    )
    out_specs = P(None, "gx", "gy", None)
    return jax.shard_map(body, mesh=mesh, in_specs=in_specs, out_specs=out_specs, check_vma=False)
```

profile of v0, /device:TPU:0, one launch (start us, length us, event | category | flops | bytes accessed | tf_op | source)
XLA Modules:
  0.0 181.6 jit_solution(16150657286715020211)
XLA Ops:
  0.0 0.0 copy-start.1
  0.7 1.3 broadcast_in_dim.18.bias_first
  2.0 1.3 broadcast_in_dim.19.bias_second
  3.3 0.7 fusion
  4.0 0.1 reshape.28
  4.1 0.1 reshape.29
  4.2 0.8 fusion.1
  5.0 0.1 reshape.30
  5.1 0.1 reshape.31
  5.2 0.1 pad_maximum_fusion
  5.3 0.8 broadcast_in_dim.20.edge_coeff_ref
  6.1 1.5 copy.17.column_ref
  7.6 1.7 reshape.36.coeff
  9.3 1.9 %copy.21.mask = s32[128,616]{1,0:T(8,128)} copy(s32[128,616]{0,1:T(8,128)} %param.25) | data formatting | bytes 630784 | tf_op args[12]
  11.2 0.0 copy-done.1
  11.2 1.5 copy.18.state_ref
  12.7 6.2 %shard_map.127 = (f32[2560,128]{1,0:T(8,128)}, f32[2,384,549]{2,1,0:T(8,128)}) custom-call(s32[1]{0:T(128)S(6)} %copy.23.count_ref, s32[512,1]{1,0:T(8,128)} %copy.17.column_ref, s32[1,512]{1,0:T(1,128)} %bitcast.11, f32[512,548]{1,0:T(8,128)} %copy.18.state_ref, f32[2,512,548]{2,1,0:T(8,128)} %bitcast.6, f32[384,1]{1,0:T(8,128)} %broadcast_in_dim.20.edge_coeff_ref), custom_call_target="tpu_custom_call" | custom-call | tf_op jit(solution)/shard_map/pallas_call | solution.py:443
  18.9 0.0 copy-start
  18.9 49.0 %shard_map.128 = (f32[2,448,549]{2,1,0:T(8,128)}, f32[128,1,2560]{2,1,0:T(1,128)}) custom-call(f32[2,384,549]{2,1,0:T(8,128)} %get-tuple-element.11.edges, f32[128,1,2560]{2,1,0:T(1,128)} %bitcast.9), custom_call_target="tpu_custom_call" | custom-call | tf_op jit(solution)/shard_map/pallas_call | solution.py:452
  67.9 0.0 copy-done
  67.9 1.8 %copy.22.out_any = f32[768,616]{1,0:T(8,128)} copy(f32[768,616]{0,1:T(8,128)S(1)} %copy-done) | data formatting | bytes 3784704 | tf_op args[7]
  69.7 73.1 %shard_map.129 = (f32[2,512,548]{2,1,0:T(8,128)}, f32[2,448,548]{2,1,0:T(8,128)}) custom-call(f32[2,512,548]{2,1,0:T(8,128)} %bitcast.7, f32[2,448,549]{2,1,0:T(8,128)} %get-tuple-element.13.halo, f32[2560,128]{1,0:T(8,128)} %bitcast.8, f32[512,1]{1,0:T(8,128)} %reshape.36.coeff, s32[128,616]{1,0:T(8,128)} %copy.21.mask, ...), custom_call_target="tpu_custom_call" | custom-call | tf_op jit(solution)/shard_map/pallas_call | solution.py:468
  142.9 34.3 %shard_map.130.landed = f32[2,448,548]{2,1,0:T(8,128)} custom-call(f32[2,448,548]{2,1,0:T(8,128)} %get-tuple-element.16.outward), custom_call_target="tpu_custom_call" | custom-call | tf_op jit(solution)/shard_map/pallas_call | solution.py:508
  177.2 4.4 %shard_map.131 = f32[2,512,548]{2,1,0:T(8,128)} custom-call(f32[2,512,548]{2,1,0:T(8,128)} %get-tuple-element.15.base, f32[2,448,548]{2,1,0:T(8,128)} %shard_map.130.landed), custom_call_target="tpu_custom_call" | custom-call | tf_op jit(solution)/shard_map/pallas_call | solution.py:517
Async XLA Ops:
  0.0 11.2 %copy-start.1 = (f32[512,548]{0,1:T(8,128)S(1)}, f32[512,548]{0,1:T(8,128)}, u32[]{:S(2)}) copy-start(f32[512,548]{0,1:T(8,128)} %param.24) | copy-start | bytes 3366916
  18.9 49.0 %copy-start = (f32[768,616]{0,1:T(8,128)S(1)}, f32[768,616]{0,1:T(8,128)}, u32[]{:S(2)}) copy-start(f32[768,616]{0,1:T(8,128)} %param.20) | copy-start | bytes 5677060
where the time goes:
time: 182 us
  Pallas kernels  167 us (92%)
  local copies, waits for them, and re-layouts  13.7 us (8%)
    pallas_call x1, Pallas kernels, body(): pl.pallas_call(functools.partial(network_kernel, tile), out_shape=(shaped...  73.1 us
    pallas_call x1, Pallas kernels, body(): pl.pallas_call(functools.partial(exchange_kernel, table), out_shape=(shap...  49 us
    pallas_call x1, Pallas kernels, body(): pl.pallas_call(functools.partial(return_kernel, table), out_shape=shaped(...  34.3 us
    pallas_call x1, Pallas kernels, body(): pl.pallas_call(functools.partial(pack_kernel, tile), out_shape=(shaped(sl...  6.19 us
    unnamed x7, local copies, waits for them, and re-layouts  5.19 us
    pallas_call x1, Pallas kernels, body(): pl.pallas_call(functools.partial(finish_kernel, tile), out_shape=shaped(p...  4.41 us

commit v1 on v0

v1 whole, which is shorter than its diff:
```python
import functools

import jax
import jax.numpy as jnp
from jax import lax
from jax.experimental import pallas as pl
from jax.experimental.pallas import tpu as pltpu
from jax.sharding import PartitionSpec as P

SWEEPS = 4
LANES = 128
GRID_WIDE = 48
GRID_LEFT = 8
F32 = jnp.float32
BF16 = jnp.bfloat16
MESH = pl.DeviceIdType.MESH
ANY = pl.BlockSpec(memory_space=pl.ANY)
VMEM = pl.BlockSpec(memory_space=pltpu.VMEM)
SMEM = pl.BlockSpec(memory_space=pltpu.SMEM)


def split(x):
    high = x.astype(BF16)
    return high, (x - high.astype(F32)).astype(BF16)


def dot(a, b, transposed=False):
    dims = (((1,), (1 if transposed else 0,)), ((), ()))
    return lax.dot_general(a, b, dims, preferred_element_type=F32)


def dot3(a, b, transposed=False):
    (ah, al), (bh, bl) = a, b
    return dot(ah, bh, transposed) + (dot(ah, bl, transposed) + dot(al, bh, transposed))


def pieces(tile_x, tile_y):
    along, across, corner = SWEEPS * tile_y, SWEEPS * tile_x, SWEEPS * SWEEPS
    first, last, left, right = 0, along, 2 * along, 2 * along + across
    low = across - corner
    sends = (
        ((1, 0), last, along),
        ((-1, 0), first, along),
        ((0, 1), right, across),
        ((0, -1), left, across),
        ((1, 1), right + low, corner),
        ((1, -1), left + low, corner),
        ((-1, 1), right, corner),
        ((-1, -1), left, corner),
    )
    table, start = [], 0
    for step, source, size in sends:
        table.append((step, source, size, start))
        start += size
    return table, start


def cell_columns(diffusivity_ref, square_ref):
    tile_x, tile_y = diffusivity_ref.shape
    square_ref[...] = jnp.zeros((LANES, LANES), F32)
    square_ref[0:tile_x, 0:tile_y] = diffusivity_ref[...]
    return jnp.transpose(square_ref[...])


def pack_kernel(tile, count_ref, row_ref, state_ref, vectors_ref, diffusivity_ref, packed_ref, edges_ref, square_ref):
    tile_x, tile_y, count_x, count_y = tile
    levels, slots = state_ref.shape
    devices = count_x * count_y
    wide = tile_y * count_y
    columns = row_ref[...]
    target = columns // wide // tile_x * count_y + columns % wide // tile_y
    cell = columns // wide % tile_x * tile_y + columns % wide % tile_y
    shape = (slots, slots)
    mine = lax.broadcasted_iota(jnp.int32, shape, 1)
    other = lax.broadcasted_iota(jnp.int32, shape, 0)
    used = count_ref[0]
    other_target = jnp.transpose(jnp.broadcast_to(target.astype(F32), (LANES, slots)))[:, 0:1]
    same = jnp.abs(other_target - target.astype(F32)) < 0.5
    earlier = same & (other < used) & (other < mine)
    ordinal = jnp.sum(earlier.astype(F32), axis=0, keepdims=True).astype(jnp.int32)
    live = lax.broadcasted_iota(jnp.int32, (1, slots), 1) < used
    place = (other == jnp.where(live, ordinal * devices + target, slots)).astype(F32)
    label = jnp.sum(place * (cell + 1).astype(F32), axis=1, keepdims=True)
    place = place.astype(BF16)
    high, rest = split(state_ref[...])
    low = (state_ref[...] - high.astype(F32) - rest.astype(F32)).astype(BF16)
    moved = dot(place, high, True) + (dot(place, rest, True) + dot(place, low, True))
    tail = levels % LANES
    parts = -(-(levels + 1) // LANES)
    bucket = slots // devices
    for part in range(parts):
        if part < parts - 1:
            block = moved[:, part * LANES : (part + 1) * LANES]
        else:
            block = jnp.concatenate(
                [
                    moved[:, part * LANES :],
                    label,
                    jnp.zeros((slots, LANES - tail - 1), F32),
                ],
                axis=1,
            )
        for turn in range(bucket):
            packed_ref[:, turn * parts + part, :] = block[turn * devices : (turn + 1) * devices]

    along, across = SWEEPS * tile_y, SWEEPS * tile_x
    cells = tile_x * tile_y
    latitude = cell_columns(diffusivity_ref, square_ref)
    for v in range(vectors_ref.shape[0]):
        edges_ref[v, 0:along, 0:levels] = vectors_ref[v, 0:along, :]
        edges_ref[v, along : 2 * along, 0:levels] = vectors_ref[v, cells - along :, :]
        for i in range(SWEEPS):
            at, last = i * tile_y, tile_x - SWEEPS + i
            edges_ref[v, at : at + tile_y, levels : levels + 1] = latitude[0:tile_y, i : i + 1]
            edges_ref[v, along + at : along + at + tile_y, levels : levels + 1] = latitude[
                0:tile_y, last : last + 1
            ]
        for i in range(tile_x):
            left = vectors_ref[v, i * tile_y : i * tile_y + SWEEPS, :]
            right = vectors_ref[v, (i + 1) * tile_y - SWEEPS : (i + 1) * tile_y, :]
            at = 2 * along + SWEEPS * i
            edges_ref[v, at : at + SWEEPS, 0:levels] = left
            edges_ref[v, at + across : at + across + SWEEPS, 0:levels] = right
            edges_ref[v, at : at + SWEEPS, levels : levels + 1] = latitude[0:SWEEPS, i : i + 1]
            edges_ref[v, at + across : at + across + SWEEPS, levels : levels + 1] = latitude[
                tile_y - SWEEPS : tile_y, i : i + 1
            ]


def piece_copies(table, source_at, target_at, sends, receives, back):
    me_x, me_y = lax.axis_index("gx"), lax.axis_index("gy")
    count_x, count_y = lax.axis_size("gx"), lax.axis_size("gy")
    sign = -1 if back else 1
    copies = []
    for k, (step, source, size, start) in enumerate(table):
        peer = {
            "gx": lax.rem(me_x + sign * step[0] + count_x, count_x),
            "gy": lax.rem(me_y + sign * step[1] + count_y, count_y),
        }
        copies.append(
            pltpu.make_async_remote_copy(
                src_ref=source_at(source, start, size),
                dst_ref=target_at(source, start, size),
                send_sem=sends.at[k],
                recv_sem=receives.at[k],
                device_id=peer,
                device_id_type=MESH,
            )
        )
    return copies


def return_copies(table, outward, landed, sends, receives, v):
    rows = lambda ref, start, size: ref.at[v, pl.ds(start, size), :]
    return piece_copies(
        table,
        lambda source, start, size: rows(outward, start, size),
        lambda source, start, size: rows(landed, start, size),
        sends.at[v],
        receives.at[v],
        True,
    )


def bucket_copy(packed, carried, source, target, send_sem, recv_sem, peer):
    count_y = lax.axis_size("gy")
    return pltpu.make_async_remote_copy(
        src_ref=packed.at[source],
        dst_ref=carried.at[target],
        send_sem=send_sem,
        recv_sem=recv_sem,
        device_id={"gx": peer // count_y, "gy": lax.rem(peer, count_y)},
        device_id_type=MESH,
    )


def spread_rows(tile_x, tile_y):
    at = lambda i, j: (i + SWEEPS) * GRID_WIDE + GRID_LEFT + j
    blocks = [(at(i, 0), tile_y) for i in range(tile_x)]
    blocks += [(at(i - SWEEPS, 0), tile_y) for i in range(SWEEPS)]
    blocks += [(at(i + tile_x, 0), tile_y) for i in range(SWEEPS)]
    blocks += [(at(i, -SWEEPS), SWEEPS) for i in range(tile_x)]
    blocks += [(at(i, tile_y), SWEEPS) for i in range(tile_x)]
    for i0 in (-SWEEPS, tile_x):
        for j0 in (-SWEEPS, tile_y):
            blocks += [(at(i0 + i, j0), SWEEPS) for i in range(SWEEPS)]
    table, start = [], 0
    for source, size in blocks:
        table.append((source, start, size))
        start += size
    return table


def network_kernel(
    tile,
    table,
    edges,
    packed,
    vectors,
    diffusivity,
    mask,
    biases,
    vertical_any,
    first_any,
    second_any,
    out_any,
    inverse_any,
    result,
    halo,
    carried,
    outward,
    landed,
    at_cells,
    square,
    vertical,
    first,
    second,
    out,
    inverse,
    grid_coeff,
    grid,
    spread,
    lifted,
    spread_high,
    spread_low,
    smooth_high,
    smooth_low,
    slope_one,
    slope_two,
    gate,
    sems,
    halo_send,
    halo_recv,
    back_send,
    back_recv,
    all_send,
    all_recv,
    own_sem,
):
    tile_x, tile_y, count_x, count_y = tile
    cells = tile_x * tile_y
    levels = vectors.shape[2]
    pairs = vectors.shape[0]
    devices = count_x * count_y
    me = lax.axis_index("gx") * count_y + lax.axis_index("gy")
    rows = lambda ref, start, size: ref.at[:, pl.ds(start, size), :]
    halo_copies = piece_copies(
        table,
        lambda source, start, size: rows(edges, source, size),
        lambda source, start, size: rows(halo, start, size),
        halo_send,
        halo_recv,
        False,
    )
    for copy in halo_copies:
        copy.start()
    own_copy = pltpu.make_async_copy(packed.at[me], carried.at[me], own_sem)
    own_copy.start()

    def send(k, carry):
        peer = lax.rem(me + k, devices)
        bucket_copy(packed, carried, peer, me, all_send, all_recv, peer).start()
        return carry

    lax.fori_loop(1, devices, send, 0)
    loads = []
    for k, (source, target) in enumerate(
        (
            (vertical_any, vertical),
            (first_any, first),
            (second_any, second),
            (out_any, out),
            (inverse_any, inverse),
        )
    ):
        load = pltpu.make_async_copy(source, target, sems.at[k])
        load.start()
        loads.append(load)

    loads[0].wait()
    loads[1].wait()
    first_split = split(first[...])
    lifted[...] = dot3(split(jnp.transpose(vertical[...])), first_split)

    for copy in halo_copies:
        copy.wait()
    latitude = cell_columns(diffusivity, square)
    order = spread_rows(tile_x, tile_y)
    grid_coeff[...] = jnp.zeros(grid_coeff.shape, F32)
    for source, start, size in order:
        if start < cells:
            column = latitude[0:tile_y, start // tile_y : start // tile_y + 1]
        else:
            column = halo[0, start - cells : start - cells + size, levels : levels + 1]
        grid_coeff[source : source + size, :] = jnp.broadcast_to(column, (size, LANES))
    chunk_x = LANES // tile_y
    near = (chunk_x + 2 * SWEEPS) * GRID_WIDE
    me_x, me_y = lax.axis_index("gx") * tile_x, lax.axis_index("gy") * tile_y
    grid[...] = jnp.zeros(grid.shape, F32)
    for q in range(tile_x // chunk_x):
        row = lax.broadcasted_iota(jnp.int32, (near, LANES), 0)
        lane = lax.broadcasted_iota(jnp.int32, (near, LANES), 1)
        i, j = row // GRID_WIDE - SWEEPS, row % GRID_WIDE - GRID_LEFT
        x, y = i + q * chunk_x + me_x, j + me_y
        inside = (x >= 0) & (x < tile_x * count_x) & (y >= 0) & (y < tile_y * count_y)
        begin = q * chunk_x * GRID_WIDE
        scale = jnp.where(inside, grid_coeff[begin : begin + near, :], 0.0)
        field = ((i == lane // tile_y) & (j == lane % tile_y)).astype(F32)
        for _ in range(SWEEPS):
            scaled = scale * field
            beside = (
                pltpu.roll(scaled, 1, 0)
                + pltpu.roll(scaled, near - 1, 0)
                + pltpu.roll(scaled, GRID_WIDE, 0)
                + pltpu.roll(scaled, near - GRID_WIDE, 0)
            )
            field = field + beside - 4.0 * scaled
        grid[begin : begin + near, q * LANES : (q + 1) * LANES] = jnp.where(inside, field, 0.0)
    for source, start, size in order:
        spread[start : start + size, :] = grid[source : source + size, :]
    total = order[-1][1] + order[-1][2]
    spread[total:, :] = jnp.zeros((spread.shape[0] - total, cells), F32)
    spread_high[...], spread_low[...] = split(spread[0:total, :])
    smooth_high[...], smooth_low[...] = split(jnp.transpose(spread[...]))

    def before(v, carry):
        own = (smooth_high[:, 0:cells], smooth_low[:, 0:cells])
        around = (smooth_high[:, cells:total], smooth_low[:, cells:total])
        smooth = dot3(own, split(vectors[v])) + dot3(around, split(halo[v, :, 0:levels]))
        at_cells[v] = dot3(split(smooth), split(lifted[...]))
        return carry

    lax.fori_loop(0, pairs, before, 0)
    own_copy.wait()
    others = pl.ds(0, devices - 1)
    bucket_copy(packed, carried, others, others, all_send, all_recv, lax.rem(me + 1, devices)).wait()

    parts = -(-(levels + 1) // LANES)
    turns = carried.shape[1] // parts
    tail = levels % LANES
    profile, label = [], []
    for turn in range(turns):
        blocks = [
            carried[:, turn * parts + part, :]
            for part in range(parts)
        ]
        label.append(blocks[-1][:, tail : tail + 1])
        profile.append(jnp.concatenate(blocks, axis=1)[:, 0:levels])
    profile = jnp.concatenate(profile, axis=0)
    slots = turns * devices
    gate_mask = jnp.transpose(mask[...].astype(F32))
    picks = []
    for turn in range(turns):
        live = (label[turn] > 0.5).astype(F32)
        gate[turn * devices : (turn + 1) * devices, :] = gate_mask * live
        across = jnp.transpose(jnp.broadcast_to(label[turn], (devices, LANES)))[0:1, :]
        picks.append(across)
    asked_row = jnp.concatenate(picks, axis=1)
    asked_column = jnp.concatenate(label, axis=0)
    number = lax.broadcasted_iota(jnp.int32, (slots, cells), 1).astype(F32) + 1.0
    pick = (jnp.abs(number - asked_column) < 0.5).astype(F32).astype(BF16)
    number = lax.broadcasted_iota(jnp.int32, (cells, slots), 0).astype(F32) + 1.0
    put = (jnp.abs(number - asked_row) < 0.5).astype(F32).astype(BF16)

    hidden = jnp.tanh(dot3(split(profile), first_split) + biases[0:1, :])
    slope_one[...] = 1.0 - hidden * hidden
    loads[2].wait()
    second_split = split(second[...])
    hidden = jnp.tanh(dot3(split(hidden), second_split) + biases[1:2, :])
    slope_two[...] = 1.0 - hidden * hidden
    loads[3].wait()
    loads[4].wait()

    def one_vector(v, carry):
        lifted_split = split(lifted[...])
        high, low = split(at_cells[v])
        tangent = (dot(pick, high) + dot(pick, low)) * slope_one[...]
        weight = split(second[...])
        tangent = dot3(split(tangent), weight) * slope_two[...]
        weight = split(out[...])
        tangent = dot3(split(tangent), weight, True) * gate[...]
        weighted = dot3(split(tangent), split(inverse[...])) * gate[...]
        gradient = dot3(split(weighted), weight) * slope_two[...]
        weight = split(second[...])
        gradient = dot3(split(gradient), weight, True) * slope_one[...]
        high, low = split(gradient)
        gradient = dot(put, high) + dot(put, low)
        gradient = split(dot3(split(gradient), lifted_split, True))
        outward[v] = dot3((spread_high[cells:total, :], spread_low[cells:total, :]), gradient)
        result[v] = vectors[v] + dot3((spread_high[0:cells, :], spread_low[0:cells, :]), gradient)
        for copy in return_copies(table, outward, landed, back_send, back_recv, v):
            copy.start()
        return carry

    lax.fori_loop(0, pairs, one_vector, 0)

    def finish(v, carry):
        for copy in return_copies(table, outward, landed, back_send, back_recv, v):
            copy.wait()
        add_landed(tile, v, landed, result)
        return carry

    lax.fori_loop(0, pairs, finish, 0)


def add_landed(tile, v, landed, result):
    tile_x, tile_y, _, _ = tile
    cells = tile_x * tile_y
    along, across = SWEEPS * tile_y, SWEEPS * tile_x
    result[v, cells - along :, :] += landed[v, 0:along, :]
    result[v, 0:along, :] += landed[v, along : 2 * along, :]
    corners = 2 * along + 2 * across
    size = SWEEPS * SWEEPS
    for i in range(tile_x):
        start = 2 * along + SWEEPS * i
        right = landed[v, start : start + SWEEPS, :]
        left = landed[v, start + across : start + across + SWEEPS, :]
        if i < SWEEPS:
            at = corners + SWEEPS * i
            left += landed[v, at + 3 * size : at + 3 * size + SWEEPS, :]
            right += landed[v, at + 2 * size : at + 2 * size + SWEEPS, :]
        if i >= tile_x - SWEEPS:
            at = corners + SWEEPS * (i - tile_x + SWEEPS)
            left += landed[v, at + size : at + size + SWEEPS, :]
            right += landed[v, at : at + SWEEPS, :]
        result[v, i * tile_y : i * tile_y + SWEEPS, :] += left
        result[v, (i + 1) * tile_y - SWEEPS : (i + 1) * tile_y, :] += right


def shaped(*shape):
    return jax.ShapeDtypeStruct(shape, F32)


LIMIT = 60 * 1024 * 1024


def body(
    vectors,
    diffusivity,
    vertical_factor,
    weight_first,
    bias_first,
    weight_second,
    bias_second,
    weight_out,
    error_inverse,
    observed_column,
    owner_count,
    observed_state,
    channel_mask,
):
    pairs, tile_x, tile_y, levels = vectors.shape
    units, channels = weight_out.shape
    count_x = lax.axis_size("gx")
    count_y = lax.axis_size("gy")
    devices = count_x * count_y
    tile = (tile_x, tile_y, count_x, count_y)
    slots = observed_column.shape[0]
    bucket = slots // devices
    cells = tile_x * tile_y
    parts = -(-(levels + 1) // LANES)
    table, halo_rows = pieces(tile_x, tile_y)
    flat = vectors.reshape(pairs, cells, levels)
    edge_rows = 2 * SWEEPS * (tile_x + tile_y)
    dma, vm = pltpu.SemaphoreType.DMA, pltpu.VMEM

    packed, edges = pl.pallas_call(
        functools.partial(pack_kernel, tile),
        out_shape=(shaped(devices, bucket * parts, LANES), shaped(pairs, edge_rows, levels + 1)),
        in_specs=[SMEM] + [VMEM] * 4,
        out_specs=(VMEM, VMEM),
        scratch_shapes=[vm((LANES, LANES), F32)],
        compiler_params=pltpu.CompilerParams(vmem_limit_bytes=LIMIT),
    )(owner_count, observed_column[None, :], observed_state.T, flat, diffusivity)

    grid_rows = (tile_x + 2 * SWEEPS) * GRID_WIDE
    total = cells + halo_rows
    padded = -(-total // LANES) * LANES
    result = pl.pallas_call(
        functools.partial(network_kernel, tile, table),
        out_shape=shaped(pairs, cells, levels),
        in_specs=[ANY] * 2 + [VMEM] * 4 + [ANY] * 5,
        out_specs=VMEM,
        scratch_shapes=[
            vm((pairs, halo_rows, levels + 1), F32),
            vm((devices, bucket * parts, LANES), F32),
            vm((pairs, halo_rows, levels), F32),
            vm((pairs, halo_rows, levels), F32),
            vm((pairs, cells, units), F32),
            vm((LANES, LANES), F32),
            vm((levels, levels), F32),
            vm((levels, units), F32),
            vm((units, units), F32),
            vm((channels, units), F32),
            vm((channels, channels), F32),
            vm((grid_rows, LANES), F32),
            vm((grid_rows, cells), F32),
            vm((padded, cells), F32),
            vm((levels, units), F32),
            vm((total, cells), BF16),
            vm((total, cells), BF16),
            vm((cells, padded), BF16),
            vm((cells, padded), BF16),
            vm((slots, units), F32),
            vm((slots, units), F32),
            vm((slots, channels), F32),
            dma((5,)),
            dma((8,)),
            dma((8,)),
            dma((pairs, 8)),
            dma((pairs, 8)),
            dma,
            dma,
            dma,
        ],
        compiler_params=pltpu.CompilerParams(vmem_limit_bytes=LIMIT, has_side_effects=True),
    )(
        edges,
        packed,
        flat,
        diffusivity,
        channel_mask.T,
        jnp.stack([bias_first, bias_second]),
        vertical_factor,
        weight_first,
        weight_second,
        weight_out.T,
        error_inverse,
    )
    return result.reshape(vectors.shape)


def solution(mesh):
    in_specs = (
        P(None, "gx", "gy", None),
        P("gx", "gy"),
        P(),
        P(),
        P(),
        P(),
        P(),
        P(),
        P(),
        P(("gx", "gy")),
        P(("gx", "gy")),
        P(("gx", "gy"), None),
        P(),
    )
    out_specs = P(None, "gx", "gy", None)
    return jax.shard_map(body, mesh=mesh, in_specs=in_specs, out_specs=out_specs, check_vma=False)
```

time: 182 us -> 135 us (0.74)
  Pallas kernels: 167 us -> 129 us
  local copies, waits for them, and re-layouts: 13.7 us -> 4.79 us
    pallas_call x5 -> x2, Pallas kernels: 167 us -> 129 us  [the longest x1 123 us: body(): pl.pallas_call(functools.partial(network_kernel, tile, table), out_shape=...]
    broadcast_in_dim x4 -> x0, local copies, waits for them, and re-layouts: 4.89 us -> none  [the longest x1 1.54 us: body(): observed_column[:, None]]
    reshape x5 -> x0, local copies, waits for them, and re-layouts: 2.02 us -> none  [the longest x1 1.68 us: body(): coeff = diffusivity.reshape(cells, 1)]
    unnamed x7 -> x1, local copies, waits for them, and re-layouts: 5.19 us -> 3.41 us
where the time goes in v1:
time: 135 us
  Pallas kernels  129 us (96%)
  local copies, waits for them, and re-layouts  4.79 us (4%)
    pallas_call x1, Pallas kernels, body(): pl.pallas_call(functools.partial(network_kernel, tile, table), out_shape=...  123 us
    pallas_call x1, Pallas kernels, body(): pl.pallas_call(functools.partial(pack_kernel, tile), out_shape=(shaped(de...  6.36 us
    unnamed x1, local copies, waits for them, and re-layouts  3.41 us

profile of v1, /device:TPU:0, one launch (start us, length us, event | category | flops | bytes accessed | tf_op | source)
XLA Modules:
  0.0 135.0 jit_solution(11370976203260396700)
XLA Ops:
  0.7 0.7 stack.9
  1.3 0.7 stack.10
  2.0 0.6 pad_maximum_fusion.biases
  2.6 6.4 %shard_map.127 = (f32[128,20,128]{2,1,0:T(8,128)}, f32[2,384,549]{2,1,0:T(8,128)}) custom-call(s32[1]{0:T(128)S(6)} %copy.15.count_ref, s32[1,512]{1,0:T(1,128)} %bitcast.12, f32[548,512]{1,0:T(8,128)} %bitcast.10, f32[2,512,548]{2,1,0:T(8,128)} %bitcast.6, f32[16,32]{1,0:T(8,128)} %diffusivity.1), custom_call_target="tpu_custom_call" | custom-call | tf_op jit(solution)/shard_map/pallas_call | solution.py:467
  9.0 122.6 %shard_map.128 = f32[2,512,548]{2,1,0:T(8,128)} custom-call(f32[2,384,549]{2,1,0:T(8,128)} %get-tuple-element.7.edges, f32[128,20,128]{2,1,0:T(8,128)} %get-tuple-element.8.packed, f32[2,512,548]{2,1,0:T(8,128)} %bitcast.7, f32[16,32]{1,0:T(8,128)} %diffusivity.1, s32[616,128]{1,0:T(8,128)} %bitcast.11, f32[2,768]{1,0:T(2,128)} %pad_maximum_fusion.biases, ...), custom_call_target="tpu_custom_call" | custom-call | tf_op jit(solution)/shard_map/pallas_call | solution.py:479
  131.6 3.4 %copy.16 = f32[2,16,32,548]{3,2,1,0:T(8,128)} copy(f32[2,16,32,548]{3,2,1,0:T(8,128)} %bitcast.8) | data formatting | bytes 4489216

commit v2 on v1

--- a/solution.py
+++ b/solution.py
@@ -36,7 +36,7 @@
 
 def pieces(tile_x, tile_y):
     along, across, corner = SWEEPS * tile_y, SWEEPS * tile_x, SWEEPS * SWEEPS
-    first, last, left, right = 0, along, 2 * along, 2 * along + across
+    first, last, left, right = 0, tile_x * tile_y - along, 0, across
     low = across - corner
     sends = (
         ((1, 0), last, along),
@@ -55,25 +55,28 @@
     return table, start
 
 
-def cell_columns(diffusivity_ref, square_ref):
-    tile_x, tile_y = diffusivity_ref.shape
-    square_ref[...] = jnp.zeros((LANES, LANES), F32)
-    square_ref[0:tile_x, 0:tile_y] = diffusivity_ref[...]
-    return jnp.transpose(square_ref[...])
-
-
-def pack_kernel(tile, count_ref, row_ref, state_ref, vectors_ref, diffusivity_ref, packed_ref, edges_ref, square_ref):
+def pack_edges(tile, vectors, edges):
+    tile_x, tile_y, _, _ = tile
+    across = SWEEPS * tile_x
+    for v in range(vectors.shape[0]):
+        for i in range(tile_x):
+            at = SWEEPS * i
+            edges[v, at : at + SWEEPS, :] = vectors[v, i * tile_y : i * tile_y + SWEEPS, :]
+            edges[v, across + at : across + at + SWEEPS, :] = vectors[
+                v, (i + 1) * tile_y - SWEEPS : (i + 1) * tile_y, :
+            ]
+
+
+def pack_profiles(tile, used, columns, state, packed):
     tile_x, tile_y, count_x, count_y = tile
-    levels, slots = state_ref.shape
+    levels, slots = state.shape
     devices = count_x * count_y
     wide = tile_y * count_y
-    columns = row_ref[...]
     target = columns // wide // tile_x * count_y + columns % wide // tile_y
     cell = columns // wide % tile_x * tile_y + columns % wide % tile_y
     shape = (slots, slots)
     mine = lax.broadcasted_iota(jnp.int32, shape, 1)
     other = lax.broadcasted_iota(jnp.int32, shape, 0)
-    used = count_ref[0]
     other_target = jnp.transpose(jnp.broadcast_to(target.astype(F32), (LANES, slots)))[:, 0:1]
     same = jnp.abs(other_target - target.astype(F32)) < 0.5
     earlier = same & (other < used) & (other < mine)
@@ -82,8 +85,8 @@
     place = (other == jnp.where(live, ordinal * devices + target, slots)).astype(F32)
     label = jnp.sum(place * (cell + 1).astype(F32), axis=1, keepdims=True)
     place = place.astype(BF16)
-    high, rest = split(state_ref[...])
-    low = (state_ref[...] - high.astype(F32) - rest.astype(F32)).astype(BF16)
+    high, rest = split(state)
+    low = (state - high.astype(F32) - rest.astype(F32)).astype(BF16)
     moved = dot(place, high, True) + (dot(place, rest, True) + dot(place, low, True))
     tail = levels % LANES
     parts = -(-(levels + 1) // LANES)
@@ -101,30 +104,7 @@
                 axis=1,
             )
         for turn in range(bucket):
-            packed_ref[:, turn * parts + part, :] = block[turn * devices : (turn + 1) * devices]
-
-    along, across = SWEEPS * tile_y, SWEEPS * tile_x
-    cells = tile_x * tile_y
-    latitude = cell_columns(diffusivity_ref, square_ref)
-    for v in range(vectors_ref.shape[0]):
-        edges_ref[v, 0:along, 0:levels] = vectors_ref[v, 0:along, :]
-        edges_ref[v, along : 2 * along, 0:levels] = vectors_ref[v, cells - along :, :]
-        for i in range(SWEEPS):
-            at, last = i * tile_y, tile_x - SWEEPS + i
-            edges_ref[v, at : at + tile_y, levels : levels + 1] = latitude[0:tile_y, i : i + 1]
-            edges_ref[v, along + at : along + at + tile_y, levels : levels + 1] = latitude[
-                0:tile_y, last : last + 1
-            ]
-        for i in range(tile_x):
-            left = vectors_ref[v, i * tile_y : i * tile_y + SWEEPS, :]
-            right = vectors_ref[v, (i + 1) * tile_y - SWEEPS : (i + 1) * tile_y, :]
-            at = 2 * along + SWEEPS * i
-            edges_ref[v, at : at + SWEEPS, 0:levels] = left
-            edges_ref[v, at + across : at + across + SWEEPS, 0:levels] = right
-            edges_ref[v, at : at + SWEEPS, levels : levels + 1] = latitude[0:SWEEPS, i : i + 1]
-            edges_ref[v, at + across : at + across + SWEEPS, levels : levels + 1] = latitude[
-                tile_y - SWEEPS : tile_y, i : i + 1
-            ]
+            packed[:, turn * parts + part, :] = block[turn * devices : (turn + 1) * devices]
 
 
 def piece_copies(table, source_at, target_at, sends, receives, back):
@@ -176,17 +156,20 @@
 
 def spread_rows(tile_x, tile_y):
     at = lambda i, j: (i + SWEEPS) * GRID_WIDE + GRID_LEFT + j
-    blocks = [(at(i, 0), tile_y) for i in range(tile_x)]
-    blocks += [(at(i - SWEEPS, 0), tile_y) for i in range(SWEEPS)]
-    blocks += [(at(i + tile_x, 0), tile_y) for i in range(SWEEPS)]
-    blocks += [(at(i, -SWEEPS), SWEEPS) for i in range(tile_x)]
-    blocks += [(at(i, tile_y), SWEEPS) for i in range(tile_x)]
-    for i0 in (-SWEEPS, tile_x):
-        for j0 in (-SWEEPS, tile_y):
-            blocks += [(at(i0 + i, j0), SWEEPS) for i in range(SWEEPS)]
+    low_x, low_y = tile_x - SWEEPS, tile_y - SWEEPS
+    blocks = [(at(i, 0), tile_y, 8, 0, i) for i in range(tile_x)]
+    blocks += [(at(i - SWEEPS, 0), tile_y, 0, 0, low_x + i) for i in range(SWEEPS)]
+    blocks += [(at(i + tile_x, 0), tile_y, 1, 0, i) for i in range(SWEEPS)]
+    blocks += [(at(i, -SWEEPS), SWEEPS, 2, low_y, i) for i in range(tile_x)]
+    blocks += [(at(i, tile_y), SWEEPS, 3, 0, i) for i in range(tile_x)]
+    slot = 4
+    for i0, from_x in ((-SWEEPS, low_x), (tile_x, 0)):
+        for j0, from_y in ((-SWEEPS, low_y), (tile_y, 0)):
+            blocks += [(at(i0 + i, j0), SWEEPS, slot, from_y, from_x + i) for i in range(SWEEPS)]
+            slot += 1
     table, start = [], 0
-    for source, size in blocks:
-        table.append((source, start, size))
+    for source, size, slot, from_y, from_x in blocks:
+        table.append((source, start, size, slot, from_y, from_x))
         start += size
     return table
 
@@ -194,9 +177,10 @@
 def network_kernel(
     tile,
     table,
-    edges,
-    packed,
-    vectors,
+    count,
+    columns,
+    state,
+    flat,
     diffusivity,
     mask,
     biases,
@@ -206,6 +190,10 @@
     out_any,
     inverse_any,
     result,
+    vectors,
+    edges,
+    packed,
+    coeffs,
     halo,
     carried,
     outward,
@@ -229,6 +217,9 @@
     slope_two,
     gate,
     sems,
+    tile_sems,
+    coeff_send,
+    coeff_recv,
     halo_send,
     halo_recv,
     back_send,
@@ -244,25 +235,40 @@
     devices = count_x * count_y
     me = lax.axis_index("gx") * count_y + lax.axis_index("gy")
     rows = lambda ref, start, size: ref.at[:, pl.ds(start, size), :]
-    halo_copies = piece_copies(
-        table,
-        lambda source, start, size: rows(edges, source, size),
-        lambda source, start, size: rows(halo, start, size),
-        halo_send,
-        halo_recv,
-        False,
-    )
-    for copy in halo_copies:
+
+    def halo_copies(part, array):
+        return piece_copies(
+            table[part],
+            lambda source, start, size: rows(array, source, size),
+            lambda source, start, size: rows(halo, start, size),
+            halo_send.at[part],
+            halo_recv.at[part],
+            False,
+        )
+
+    coeff_copies = []
+    for k, entry in enumerate(table):
+        coeff_copies += piece_copies(
+            [entry],
+            lambda source, start, size: diffusivity,
+            lambda source, start, size, k=k: coeffs.at[k],
+            coeff_send.at[k : k + 1],
+            coeff_recv.at[k : k + 1],
+            False,
+        )
+    far_copies = halo_copies(slice(0, 2), flat)
+    for copy in coeff_copies + far_copies:
         copy.start()
-    own_copy = pltpu.make_async_copy(packed.at[me], carried.at[me], own_sem)
-    own_copy.start()
+    own_coeff = pltpu.make_async_copy(diffusivity, coeffs.at[8], tile_sems.at[0])
+    own_coeff.start()
+    own_tile = pltpu.make_async_copy(flat, vectors, tile_sems.at[1])
+    own_tile.start()
 
     def send(k, carry):
         peer = lax.rem(me + k, devices)
         bucket_copy(packed, carried, peer, me, all_send, all_recv, peer).start()
         return carry
 
-    lax.fori_loop(1, devices, send, 0)
     loads = []
     for k, (source, target) in enumerate(
         (
@@ -277,21 +283,32 @@
         load.start()
         loads.append(load)
 
+    own_tile.wait()
+    pack_edges(tile, vectors, edges)
+    pack_profiles(tile, count[0], columns[...], state[...], packed)
+    near_copies = halo_copies(slice(2, 8), edges)
+    for copy in near_copies:
+        copy.start()
     loads[0].wait()
     loads[1].wait()
     first_split = split(first[...])
     lifted[...] = dot3(split(jnp.transpose(vertical[...])), first_split)
 
-    for copy in halo_copies:
+    own_copy = pltpu.make_async_copy(packed.at[me], carried.at[me], own_sem)
+    own_copy.start()
+    lax.fori_loop(1, devices, send, 0)
+    own_coeff.wait()
+    for copy in coeff_copies:
         copy.wait()
-    latitude = cell_columns(diffusivity, square)
     order = spread_rows(tile_x, tile_y)
+    square[...] = jnp.zeros((LANES, LANES), F32)
+    latitude = []
+    for slot in range(9):
+        square[0:tile_x, 0:tile_y] = coeffs[slot]
+        latitude.append(jnp.transpose(square[...]))
     grid_coeff[...] = jnp.zeros(grid_coeff.shape, F32)
-    for source, start, size in order:
-        if start < cells:
-            column = latitude[0:tile_y, start // tile_y : start // tile_y + 1]
-        else:
-            column = halo[0, start - cells : start - cells + size, levels : levels + 1]
+    for source, start, size, slot, from_y, from_x in order:
+        column = latitude[slot][from_y : from_y + size, from_x : from_x + 1]
         grid_coeff[source : source + size, :] = jnp.broadcast_to(column, (size, LANES))
     chunk_x = LANES // tile_y
     near = (chunk_x + 2 * SWEEPS) * GRID_WIDE
@@ -316,12 +333,15 @@
             )
             field = field + beside - 4.0 * scaled
         grid[begin : begin + near, q * LANES : (q + 1) * LANES] = jnp.where(inside, field, 0.0)
-    for source, start, size in order:
+    for source, start, size, _, _, _ in order:
         spread[start : start + size, :] = grid[source : source + size, :]
     total = order[-1][1] + order[-1][2]
     spread[total:, :] = jnp.zeros((spread.shape[0] - total, cells), F32)
     spread_high[...], spread_low[...] = split(spread[0:total, :])
     smooth_high[...], smooth_low[...] = split(jnp.transpose(spread[...]))
+
+    for copy in far_copies + near_copies:
+        copy.wait()
 
     def before(v, carry):
         own = (smooth_high[:, 0:cells], smooth_low[:, 0:cells])
@@ -461,28 +481,21 @@
     parts = -(-(levels + 1) // LANES)
     table, halo_rows = pieces(tile_x, tile_y)
     flat = vectors.reshape(pairs, cells, levels)
-    edge_rows = 2 * SWEEPS * (tile_x + tile_y)
     dma, vm = pltpu.SemaphoreType.DMA, pltpu.VMEM
-
-    packed, edges = pl.pallas_call(
-        functools.partial(pack_kernel, tile),
-        out_shape=(shaped(devices, bucket * parts, LANES), shaped(pairs, edge_rows, levels + 1)),
-        in_specs=[SMEM] + [VMEM] * 4,
-        out_specs=(VMEM, VMEM),
-        scratch_shapes=[vm((LANES, LANES), F32)],
-        compiler_params=pltpu.CompilerParams(vmem_limit_bytes=LIMIT),
-    )(owner_count, observed_column[None, :], observed_state.T, flat, diffusivity)
-
     grid_rows = (tile_x + 2 * SWEEPS) * GRID_WIDE
     total = cells + halo_rows
     padded = -(-total // LANES) * LANES
     result = pl.pallas_call(
         functools.partial(network_kernel, tile, table),
         out_shape=shaped(pairs, cells, levels),
-        in_specs=[ANY] * 2 + [VMEM] * 4 + [ANY] * 5,
+        in_specs=[SMEM] + [VMEM] * 2 + [ANY] * 2 + [VMEM] * 2 + [ANY] * 5,
         out_specs=VMEM,
         scratch_shapes=[
-            vm((pairs, halo_rows, levels + 1), F32),
+            vm((pairs, cells, levels), F32),
+            vm((pairs, 2 * SWEEPS * tile_x, levels), F32),
+            vm((devices, bucket * parts, LANES), F32),
+            vm((9, tile_x, tile_y), F32),
+            vm((pairs, halo_rows, levels), F32),
             vm((devices, bucket * parts, LANES), F32),
             vm((pairs, halo_rows, levels), F32),
             vm((pairs, halo_rows, levels), F32),
@@ -505,6 +518,9 @@
             vm((slots, units), F32),
             vm((slots, channels), F32),
             dma((5,)),
+            dma((2,)),
+            dma((8,)),
+            dma((8,)),
             dma((8,)),
             dma((8,)),
             dma((pairs, 8)),
@@ -515,8 +531,9 @@
         ],
         compiler_params=pltpu.CompilerParams(vmem_limit_bytes=LIMIT, has_side_effects=True),
     )(
-        edges,
-        packed,
+        owner_count,
+        observed_column[None, :],
+        observed_state.T,
         flat,
         diffusivity,
         channel_mask.T,

time: 135 us -> 128 us (0.948); the launches traced: 135 us -> 127 us
  Pallas kernels: 129 us -> 121 us
    pallas_call x1 -> x0, Pallas kernels: 6.36 us -> none  [body(): pl.pallas_call(functools.partial(pack_kernel, tile), out_shape=(shaped(de...]
    pallas_call x1, Pallas kernels: 123 us -> 121 us  [body(): pl.pallas_call(functools.partial(network_kernel, tile, table), out_shape=...]
where the time goes in v2:
time: 128 us; the launch traced here: 127 us
  Pallas kernels  121 us (95%)
  local copies, waits for them, and re-layouts  4.79 us (4%)
    pallas_call x1, Pallas kernels, body(): pl.pallas_call(functools.partial(network_kernel, tile, table), out_shape=...  121 us
    unnamed x1, local copies, waits for them, and re-layouts  3.41 us

profile of v2, /device:TPU:0, one launch (start us, length us, event | category | flops | bytes accessed | tf_op | source)
XLA Modules:
  0.0 126.6 jit_solution(9438782434866636871)
XLA Ops:
  0.7 0.7 stack.9
  1.3 0.7 stack.10
  2.0 0.6 pad_maximum_fusion.biases
  2.6 120.6 %shard_map.127 = f32[2,512,548]{2,1,0:T(8,128)} custom-call(s32[1]{0:T(128)S(6)} %copy.15.count, s32[1,512]{1,0:T(1,128)} %bitcast.11, f32[548,512]{1,0:T(8,128)} %bitcast.9, f32[2,512,548]{2,1,0:T(8,128)} %bitcast.7, f32[16,32]{1,0:T(8,128)} %diffusivity.1, s32[616,128]{1,0:T(8,128)} %bitcast.10, f32[2,768]{1,0:T(2,128)} %pad_maximum_fusion.biases, ...), custom_call_target="tpu_custom_call" | custom-call | tf_op jit(solution)/shard_map/pallas_call | solution.py:488
  123.2 3.4 %copy.16 = f32[2,16,32,548]{3,2,1,0:T(8,128)} copy(f32[2,16,32,548]{3,2,1,0:T(8,128)} %bitcast.6) | data formatting | bytes 4489216

commit v3 on v2

--- a/solution.py
+++ b/solution.py
@@ -154,6 +154,10 @@
     )
 
 
+def one_row(ref):
+    return jnp.concatenate([ref[i : i + 1, :] for i in range(ref.shape[0])], axis=1)
+
+
 def spread_rows(tile_x, tile_y):
     at = lambda i, j: (i + SWEEPS) * GRID_WIDE + GRID_LEFT + j
     low_x, low_y = tile_x - SWEEPS, tile_y - SWEEPS
@@ -183,7 +187,8 @@
     flat,
     diffusivity,
     mask,
-    biases,
+    bias_first,
+    bias_second,
     vertical_any,
     first_any,
     second_any,
@@ -382,11 +387,11 @@
     number = lax.broadcasted_iota(jnp.int32, (cells, slots), 0).astype(F32) + 1.0
     put = (jnp.abs(number - asked_row) < 0.5).astype(F32).astype(BF16)
 
-    hidden = jnp.tanh(dot3(split(profile), first_split) + biases[0:1, :])
+    hidden = jnp.tanh(dot3(split(profile), first_split) + one_row(bias_first))
     slope_one[...] = 1.0 - hidden * hidden
     loads[2].wait()
     second_split = split(second[...])
-    hidden = jnp.tanh(dot3(split(hidden), second_split) + biases[1:2, :])
+    hidden = jnp.tanh(dot3(split(hidden), second_split) + one_row(bias_second))
     slope_two[...] = 1.0 - hidden * hidden
     loads[3].wait()
     loads[4].wait()
@@ -488,7 +493,7 @@
     result = pl.pallas_call(
         functools.partial(network_kernel, tile, table),
         out_shape=shaped(pairs, cells, levels),
-        in_specs=[SMEM] + [VMEM] * 2 + [ANY] * 2 + [VMEM] * 2 + [ANY] * 5,
+        in_specs=[SMEM] + [VMEM] * 2 + [ANY] * 2 + [VMEM] * 3 + [ANY] * 5,
         out_specs=VMEM,
         scratch_shapes=[
             vm((pairs, cells, levels), F32),
@@ -537,7 +542,8 @@
         flat,
         diffusivity,
         channel_mask.T,
-        jnp.stack([bias_first, bias_second]),
+        bias_first.reshape(-1, LANES),
+        bias_second.reshape(-1, LANES),
         vertical_factor,
         weight_first,
         weight_second,

time: 128 us -> 126 us (0.984)
  local copies, waits for them, and re-layouts: 4.79 us -> 3.41 us
    another operation x2 -> x0, local copies, waits for them, and re-layouts: 1.38 us -> none  [body(): jnp.stack([bias_first, bias_second])]
where the time goes in v3:
time: 126 us; the launch traced here: 125 us
  Pallas kernels  121 us (96%)
  local copies, waits for them, and re-layouts  3.41 us (3%)
    pallas_call x1, Pallas kernels, body(): pl.pallas_call(functools.partial(network_kernel, tile, table), out_shape=...  121 us
    unnamed x1, local copies, waits for them, and re-layouts  3.41 us

profile of v3, /device:TPU:0, one launch (start us, length us, event | category | flops | bytes accessed | tf_op | source)
XLA Modules:
  0.0 124.8 jit_solution(8183520173638902731)
XLA Ops:
  0.7 120.7 %shard_map.127 = f32[2,512,548]{2,1,0:T(8,128)} custom-call(s32[1]{0:T(128)S(6)} %copy.15.count, s32[1,512]{1,0:T(1,128)} %bitcast.15, f32[548,512]{1,0:T(8,128)} %bitcast.11, f32[2,512,548]{2,1,0:T(8,128)} %bitcast.9, f32[16,32]{1,0:T(8,128)} %diffusivity.1, s32[616,128]{1,0:T(8,128)} %bitcast.12, f32[6,128]{1,0:T(8,128)} %bitcast.13, f32[6,128]{1,0:T(8,128)} %bitcast.14, ...), custom_call_target="tpu_custom_call" | custom-call | tf_op jit(solution)/shard_map/pallas_call | solution.py:493
  121.4 3.4 %copy.16 = f32[2,16,32,548]{3,2,1,0:T(8,128)} copy(f32[2,16,32,548]{3,2,1,0:T(8,128)} %bitcast.8) | data formatting | bytes 4489216
